TPU v7x, 128 devices: a whole 4x4x4 slice. The times are simulated.
128 devices in a mesh: batch: 1, g: 128 (over z, y, x, core).
Axes of the slice: x: 4, y: 4, z: 4, core: 2. Of those that a mesh axis runs over, the one named last changes fastest.
Arguments:
- keys: float32 [131072], P(('batch', 'g'))
- payload: bfloat16 [131072, 896], P(('batch', 'g'))
Outputs:
- output 1: float32 [262144], P(('batch', 'g'))
- output 2: bfloat16 [262144, 896], P(('batch', 'g'))
- output 3: int32 [128], P(('batch', 'g'))
All inputs are finite; a program needn't handle non-finite values.
Results may differ from a plain program's by a relative error of at most 0.001.
Values are sent between devices in bfloat16 or wider.
A program may use at most 1 GiB of HBM per device.

v0:
```python
import jax
import jax.numpy as jnp
from jax import lax
from jax.sharding import PartitionSpec as P

PAD_KEY = 128.0


def solution(mesh):
    group_size = mesh.shape["g"]

    def local_part(keys_loc, rows_loc):
        n_dev = keys_loc.shape[0]
        width = rows_loc.shape[1]
        cap_rows = 2 * n_dev // group_size
        sorted_keys, sort_order = lax.sort((keys_loc, lax.iota(jnp.int32, n_dev)), num_keys=1)
        samples = sorted_keys[:: n_dev // group_size]
        all_samples = jnp.sort(lax.all_gather(samples, "g", tiled=True))
        splitters = all_samples[group_size + group_size // 2 :: group_size]
        edges = jnp.searchsorted(sorted_keys, splitters, side="left").astype(jnp.int32)
        starts = jnp.concatenate([jnp.zeros((1,), jnp.int32), edges])
        stops = jnp.concatenate([edges, jnp.full((1,), n_dev, jnp.int32)])
        src_pos = starts[:, None] + lax.iota(jnp.int32, cap_rows)[None, :]
        is_valid = src_pos < stops[:, None]
        src_pos = jnp.minimum(src_pos, n_dev - 1)
        send_keys = jnp.where(is_valid, sorted_keys[src_pos], PAD_KEY)
        send_rows = jnp.where(is_valid[:, :, None], rows_loc[sort_order[src_pos]], 0.0)
        recv_keys = lax.all_to_all(send_keys, "g", 0, 0, tiled=True)
        recv_rows = lax.all_to_all(send_rows, "g", 0, 0, tiled=True)
        flat_keys = recv_keys.reshape(-1)
        merged_keys, merge_order = lax.sort((flat_keys, lax.iota(jnp.int32, flat_keys.shape[0])), num_keys=1)
        merged_rows = recv_rows.reshape(-1, width)[merge_order]
        own_count = jnp.sum(flat_keys < PAD_KEY).astype(jnp.int32).reshape(1)
        return merged_keys, merged_rows, own_count

    row_spec = P(("batch", "g"))
    mat_spec = P(("batch", "g"), None)
    return jax.shard_map(local_part, mesh=mesh, in_specs=(row_spec, mat_spec), out_specs=(row_spec, mat_spec, row_spec), check_vma=False)
```

profile of v0, /device:TPU:1, one launch (start us, length us, event | category | flops | bytes accessed | tf_op | source)
XLA Modules:
  0.0 175.7 jit_solution(366516593244573825)
XLA Ops:
  0.6 0.0 copy-start
  0.7 4.7 %sort.45 = (f32[1024]{0:T(1024)S(1)}, s32[1024]{0:T(1024)S(1)}) sort(f32[1024]{0:T(1024)} %param.4, s32[1024]{0:T(1024)S(1)} %iota.22), dimensions={0}, to_apply=%region_0.0 | sort | flops 10240 | bytes 16384 | tf_op jit(solution)/shard_map/sort | solution.py:16
  5.4 0.2 slice.6
  5.6 38.7 %all-gather = f32[128,1,128]{2,1,0:T(1,128)S(1)} all-gather(f32[1,1,128]{2,1,0:T(1,128)S(1)} %bitcast.14), channel_id=1, replica_groups=mesh['batch'=1,'g'=128] {'g'}, dimensions={0}, use_global_device_ids=true | all-gather | bytes 66048 | tf_op jit(solution)/shard_map/all_gather | solution.py:18
  44.4 8.7 %sort.46 = (f32[16384]{0:T(1024)S(1)}, s32[16384]{0:T(1024)}) sort(f32[16384]{0:T(1024)S(1)} %bitcast.13, s32[16384]{0:T(1024)S(1)} %iota.23), dimensions={0}, to_apply=%region_1.0 | sort | flops 229376 | bytes 262144 | tf_op jit(solution)/shard_map/jit(sort)/sort | solution.py:18
  53.1 0.2 slice.7
  53.3 11.8 %while.24 = (s32[]{:T(128)}, u32[127]{0:T(128)S(1)}, u32[127]{0:T(128)S(1)}, f32[127]{0:T(128)S(1)}, pred[127]{0:T(512)(128)(4,1)S(1)}, /*index=5*/f32[1024]{0:T(1024)S(1)}, s32[]{:T(128)}, s32[]{:T(128)}, s32[]{}) while((s32[]{:T(128)}, u32[127]{0:T(128)S(1)}, u32[127]{0:T(128)S(1)}, f32[127]{0:T(128)S(1)}, ...), condition=%wide.region_3.4_spmd.clone, body=%wide.region_2.3_spmd.clone.sunk | while | flops 5219 | bytes 13230 | solution.py:20
  53.4 1.0 gather_fusion
  54.4 1.0 gather_fusion
  55.5 1.0 gather_fusion
  56.6 1.0 gather_fusion
  57.6 1.0 gather_fusion
  58.7 1.0 gather_fusion
  59.8 1.0 gather_fusion
  60.9 1.0 gather_fusion
  61.9 1.0 gather_fusion
  63.0 1.0 gather_fusion
  64.1 1.0 gather_fusion
  65.1 0.1 pad_add_fusion.1
  65.2 0.1 compare_select_fusion.6
  65.3 0.1 reshape.174
  65.4 8.6 %gather_fusion.1 = f32[2048]{0:T(1024)S(1)} fusion(f32[1024]{0:T(1024)S(1)} %get-tuple-element.191, s32[2048]{0:T(1024)S(1)} %broadcast_clamp_fusion.1), kind=kCustom, calls=%fused_computation.1 | custom fusion | bytes 24576 | tf_op jit(solution)/shard_map/gather | solution.py:26
  74.0 0.1 gather.23
  74.0 0.7 fusion.5
  74.8 5.9 %all-to-all-start = ((f32[128,1,16]{2,1,0:T(1,128)}), f32[128,1,16]{2,1,0:T(1,128)S(1)}, u32[]{:S(2)}, u32[]{:S(2)}) async-start(f32[128,1,16]{2,1,0:T(1,128)} %bitcast.2), calls=%async_computation | async-start | bytes 131072 | tf_op jit(solution)/shard_map/all_to_all | solution.py:28
  80.6 0.1 add_compare_fusion
  80.7 8.6 %gather_fusion.2 = s32[2048]{0:T(1024)S(1)} fusion(s32[1024]{0:T(1024)S(1)} %get-tuple-element.84, s32[2048]{0:T(1024)S(1)} %broadcast_clamp_fusion.1), kind=kCustom, calls=%fused_computation.2 | custom fusion | bytes 24576 | tf_op jit(solution)/shard_map/gather | solution.py:27
  89.3 0.1 gather.25
  89.4 0.1 reshape.190
  89.5 0.0 copy-done
  89.5 9.5 %gather_fusion.3 = bf16[2048,896]{1,0:T(8,128)(2,1)} fusion(bf16[1024,896]{1,0:T(8,128)(2,1)S(1)} %copy-done, s32[2048]{0:T(1024)S(1)} %broadcast_clamp_fusion), kind=kCustom, calls=%fused_computation.3 | custom fusion | bytes 7348224 | tf_op jit(solution)/shard_map/gather | solution.py:27
  99.0 3.6 %broadcast_select_fusion.2 = bf16[128,16,896]{2,1,0:T(8,128)(2,1)} fusion(bf16[128,16,896]{2,1,0:T(8,128)(2,1)} %bitcast.11, pred[128,16]{1,0:T(8,128)(4,1)S(1)} %add_compare_fusion), kind=kLoop, calls=%fused_computation.19 | loop fusion | flops 1835008 | bytes 7342080 | tf_op jit(solution)/shard_map/jit(_where)/select_n | solution.py:27
  102.6 0.0 all-to-all-done
  102.6 10.2 %all-to-all-start.1 = ((bf16[128,16,896]{2,1,0:T(8,128)(2,1)}), bf16[128,16,896]{2,1,0:T(8,128)(2,1)}, u32[]{:S(2)}, u32[]{:S(2)}) async-start(bf16[128,16,896]{2,1,0:T(8,128)(2,1)} %broadcast_select_fusion.2), calls=%async_computation.1 | async-start | bytes 7340032 | tf_op jit(solution)/shard_map/all_to_all | solution.py:29
  112.8 0.5 broadcast.235
  113.3 0.8 reduce.5
  114.1 0.1 reshape.161
  114.2 5.2 %sort.47 = (f32[2048]{0:T(1024)}, s32[2048]{0:T(1024)S(1)}) sort(f32[2048]{0:T(1024)S(1)} %reshape.161, s32[2048]{0:T(1024)S(1)} %iota.24), dimensions={0}, to_apply=%region_4.5 | sort | flops 22528 | bytes 32768 | tf_op jit(solution)/shard_map/sort | solution.py:31
  119.5 0.6 convert_reduce_fusion
  120.1 42.7 %all-to-all-done.1 = bf16[128,16,896]{2,1,0:T(8,128)(2,1)} async-done(((bf16[128,16,896]{2,1,0:T(8,128)(2,1)}), bf16[128,16,896]{2,1,0:T(8,128)(2,1)}, u32[]{:S(2)}, u32[]{:S(2)}) %all-to-all-start.1) | async-done | bytes 3670048 | tf_op jit(solution)/shard_map/all_to_all | solution.py:29
  162.8 12.9 %gather_fusion.4 = bf16[2048,896]{1,0:T(8,128)(2,1)} fusion(bf16[2048,896]{1,0:T(8,128)(2,1)} %bitcast.4, s32[2048]{0:T(1024)S(1)} %fusion.6), kind=kCustom, calls=%fused_computation.4 | custom fusion | bytes 7348224 | tf_op jit(solution)/shard_map/gather | solution.py:32
  (66 shorter events, 0.5 us)
Async XLA Ops:
  0.6 88.9 %copy-start = (bf16[1024,896]{1,0:T(8,128)(2,1)S(1)}, bf16[1024,896]{1,0:T(8,128)(2,1)}, u32[]{:S(2)}) copy-start(bf16[1024,896]{1,0:T(8,128)(2,1)} %param.5) | copy-start | bytes 5505028
  74.8 27.9 %all-to-all-start = ((f32[128,1,16]{2,1,0:T(1,128)}), f32[128,1,16]{2,1,0:T(1,128)S(1)}, u32[]{:S(2)}, u32[]{:S(2)}) async-start(f32[128,1,16]{2,1,0:T(1,128)} %bitcast.2), calls=%async_computation | async-start | bytes 131072 | tf_op jit(solution)/shard_map/all_to_all | solution.py:28
  102.6 60.2 %all-to-all-start.1 = ((bf16[128,16,896]{2,1,0:T(8,128)(2,1)}), bf16[128,16,896]{2,1,0:T(8,128)(2,1)}, u32[]{:S(2)}, u32[]{:S(2)}) async-start(bf16[128,16,896]{2,1,0:T(8,128)(2,1)} %broadcast_select_fusion.2), calls=%async_computation.1 | async-start | bytes 7340032 | tf_op jit(solution)/shard_map/all_to_all | solution.py:29
where the time goes:
time: 178 us; the launch traced here: 176 us
  local copies, waits for them, and re-layouts  51.6 us (29%)
  waiting for transfers between devices  42.7 us (24%)
  blocking collectives  38.7 us (22%)
  other arithmetic  25.3 us (14%)
  starting transfers between devices  16 us (9%)
    all_to_all x1, waiting for transfers between devices, local_part(): recv_rows = lax.all_to_all(send_rows, 'g', 0, 0, tiled=True)  42.7 us
    all_gather x1, blocking collectives, local_part(): all_samples = jnp.sort(lax.all_gather(samples, 'g', tiled=True))  38.7 us
    gather x1, local copies, waits for them, and re-layouts, local_part(): merged_rows = recv_rows.reshape(-1, width)[merge_order]  12.9 us
    gather x11, local copies, waits for them, and re-layouts, local_part(): jnp.searchsorted(sorted_keys, splitters, side='left').astype(jnp.int32)  10.7 us
    all_to_all x1, starting transfers between devices, local_part(): recv_rows = lax.all_to_all(send_rows, 'g', 0, 0, tiled=True)  10.2 us
    gather x1, local copies, waits for them, and re-layouts, local_part(): rows_loc[sort_order[src_pos]]  9.47 us
    sort x1, other arithmetic, local_part(): all_samples = jnp.sort(lax.all_gather(samples, 'g', tiled=True))  8.73 us
    gather x2, local copies, waits for them, and re-layouts, local_part(): sort_order[src_pos]  8.66 us
  transfers between devices with their start and end apart: 2, of which 1 were waited for; matrix products, arithmetic and copies ran while one was open for 17% of the time, Pallas kernels for 0%

commit v1 on v0

v1 whole, which is shorter than its diff:
```python
import functools
import jax
import jax.numpy as jnp
from jax import lax
from jax.sharding import PartitionSpec as P
from jax.experimental import pallas as pl
from jax.experimental.pallas import tpu as pltpu

PAD_KEY = 128.0
G = 128
N = 1024
W = 896
T = 7
CAP = 16
OUT = 2048
MESH = pl.DeviceIdType.MESH


def lane_iota(shape):
    return lax.broadcasted_iota(jnp.int32, shape, 1)


def sub_iota(shape):
    return lax.broadcasted_iota(jnp.int32, shape, 0)


def exchange_kernel(
    keys_ref, pay_hbm, rk_ref, rows_hbm,
    pay_b, pay_f, stage, sendbuf, samp, runs, kbuf, rk, srt, tab_v, st_v, tab_s, st_s,
    in_sem, tab_sem, self_sem, s_send, s_recv, k_send, k_recv, p_send, p_recv,
):
    me = lax.axis_index("g")
    barrier = pltpu.get_barrier_semaphore()

    def peer(k):
        return lax.rem(me + k, G)

    def greet(k, c):
        pl.semaphore_signal(barrier, inc=1, device_id={"g": peer(k)}, device_id_type=MESH)
        return c

    load = pltpu.make_async_copy(pay_hbm, pay_b, in_sem)
    load.start()
    lax.fori_loop(1, G, greet, 0)

    keys = keys_ref[...]
    keys_t = jnp.transpose(keys)
    rank_cols = []
    for a in range(8):
        col = keys_t[:, a : a + 1]
        acc = jnp.zeros((G, 128), jnp.int32)
        for b in range(8):
            acc = acc + (keys[b : b + 1, :] < col).astype(jnp.int32)
        rank_cols.append(jnp.sum(acc, axis=1, keepdims=True))
    samples = jnp.zeros((1, 128), jnp.float32)
    for a in range(8):
        hit = rank_cols[a] == lane_iota((G, 128)) * 8
        samples = samples + jnp.sum(jnp.where(hit, keys_t[:, a : a + 1], 0.0), axis=0, keepdims=True)
    samp[...] = samples
    for r in range(8):
        want = lane_iota((G, 128)) + r * 128
        ks = jnp.zeros((G, 128), jnp.float32)
        ps = jnp.zeros((G, 128), jnp.int32)
        for a in range(8):
            hit = rank_cols[a] == want
            src = sub_iota((G, 128)) + a * 128
            addr = (src >> 3) * (8 * T) + (src & 7)
            ks = ks + jnp.where(hit, keys_t[:, a : a + 1], 0.0)
            ps = ps + jnp.where(hit, addr, 0)
        srt[r : r + 1, :] = jnp.sum(ks, axis=0, keepdims=True)
        tab_v[r : r + 1, :] = jnp.sum(ps, axis=0, keepdims=True)
    tab_v[8:16, :] = jnp.zeros((8, 128), jnp.int32)
    tab_copy = pltpu.make_async_copy(tab_v, tab_s, tab_sem)
    tab_copy.start()

    pl.semaphore_wait(barrier, G - 1)

    def send_samples(k, c):
        pltpu.make_async_remote_copy(
            src_ref=samp, dst_ref=runs.at[pl.ds(me, 1), :], send_sem=s_send, recv_sem=s_recv,
            device_id={"g": peer(k)}, device_id_type=MESH,
        ).start()
        return c

    lax.fori_loop(1, G, send_samples, 0)

    load.wait()

    def widen(g, c):
        x = pay_b[pl.ds(pl.multiple_of(g * 16, 16), 16), :].astype(jnp.float32)
        base = pl.multiple_of(g * (16 * T), 16)
        for h in range(2):
            for t in range(T):
                pay_f[pl.ds(base + h * 8 * T + t * 8, 8), :] = x[h * 8 : h * 8 + 8, t * 128 : t * 128 + 128]
        return c

    lax.fori_loop(0, N // 16, widen, 0)
    tab_copy.wait()

    pltpu.make_async_copy(runs.at[pl.ds(0, G - 1), :], runs.at[pl.ds(0, G - 1), :], s_recv).wait()
    pltpu.make_async_copy(runs.at[pl.ds(0, G - 1), :], runs.at[pl.ds(0, G - 1), :], s_send).wait()
    runs[pl.ds(me, 1), :] = samp[...]

    queries = [jnp.broadcast_to(srt[b : b + 1, :], (8, 128)) for b in range(8)]

    def count(sg, accs):
        run = runs[pl.ds(pl.multiple_of(sg * 8, 8), 8), :]
        out = []
        for b in range(8):
            pos = jnp.zeros((8, 128), jnp.int32)
            for step in (64, 32, 16, 8, 4, 2, 1, 1):
                v = jnp.take_along_axis(run, pos + (step - 1), axis=1)
                pos = pos + jnp.where(v <= queries[b], step, 0)
            out.append(accs[b] + pos)
        return tuple(out)

    accs = lax.fori_loop(0, 16, count, tuple(jnp.zeros((8, 128), jnp.int32) for _ in range(8)))
    reach = jnp.concatenate([jnp.sum(a, axis=0, keepdims=True) for a in accs], axis=0)
    reach_t = jnp.transpose(reach)
    lanes = lane_iota((G, 128))
    lo = jnp.where(lanes == 0, 0, lanes * 128 + 65)
    hi = jnp.where(lanes == 127, 1 << 20, lanes * 128 + (128 + 65))
    start = jnp.zeros((G, 128), jnp.int32)
    stop = jnp.zeros((G, 128), jnp.int32)
    for b in range(8):
        col = reach_t[:, b : b + 1]
        start = start + (col < lo).astype(jnp.int32)
        stop = stop + (col < hi).astype(jnp.int32)
    start = jnp.sum(start, axis=0, keepdims=True)
    stop = jnp.sum(stop, axis=0, keepdims=True)
    st_v[...] = start
    st_copy = pltpu.make_async_copy(st_v, st_s, tab_sem)
    st_copy.start()

    pair_t = jnp.transpose(jnp.concatenate([start, stop, jnp.zeros((6, 128), jnp.int32)], axis=0))
    tables = [jnp.broadcast_to(srt[b : b + 1, :], (8, 128)) for b in range(8)]
    for dg in range(16):
        first = pair_t[dg * 8 : dg * 8 + 8, 0:1]
        last = pair_t[dg * 8 : dg * 8 + 8, 1:2]
        slot = lane_iota((8, 128))
        idx = first + slot
        pick = idx & 127
        part = idx >> 7
        val = jnp.full((8, 128), PAD_KEY, jnp.float32)
        for b in range(8):
            val = jnp.where(part == b, jnp.take_along_axis(tables[b], pick, axis=1), val)
        kbuf[dg * 8 : dg * 8 + 8, :] = jnp.where((idx < last) & (slot < CAP), val, PAD_KEY)

    def send_keys(k, c):
        p = peer(k)
        pltpu.make_async_remote_copy(
            src_ref=kbuf.at[pl.ds(p, 1), :], dst_ref=rk.at[pl.ds(me, 1), :], send_sem=k_send, recv_sem=k_recv,
            device_id={"g": p}, device_id_type=MESH,
        ).start()
        return c

    lax.fori_loop(1, G, send_keys, 0)
    st_copy.wait()

    def build(d):
        first = st_s[0, d]
        for t in range(CAP):
            pos = first + t
            addr = tab_s[pos >> 7, pos & 127]
            stage[pl.ds((t // 8) * 8 * T + (t % 8), T, stride=8), :] = pay_f[pl.ds(addr, T, stride=8), :]
        for c in range(T):
            block = jnp.concatenate(
                [stage[c * 8 : c * 8 + 8, :], stage[8 * T + c * 8 : 8 * T + c * 8 + 8, :]], axis=0)
            sendbuf[d, :, c * 128 : c * 128 + 128] = block.astype(jnp.bfloat16)

    def send_rows(k, c):
        p = peer(k)
        build(p)
        pltpu.make_async_remote_copy(
            src_ref=sendbuf.at[p], dst_ref=rows_hbm.at[me], send_sem=p_send, recv_sem=p_recv,
            device_id={"g": p}, device_id_type=MESH,
        ).start()
        return c

    lax.fori_loop(1, G, send_rows, 0)
    build(me)
    own = pltpu.make_async_copy(sendbuf.at[me], rows_hbm.at[me], self_sem)
    own.start()
    own.wait()

    pltpu.make_async_copy(rk.at[pl.ds(0, G - 1), :], rk.at[pl.ds(0, G - 1), :], k_recv).wait()
    pltpu.make_async_copy(rk.at[pl.ds(0, G - 1), :], rk.at[pl.ds(0, G - 1), :], k_send).wait()
    rk[pl.ds(me, 1), :] = kbuf[pl.ds(me, 1), :]
    rk_ref[...] = rk[...]
    pltpu.make_async_copy(rows_hbm.at[pl.ds(0, G - 1)], rows_hbm.at[pl.ds(0, G - 1)], p_recv).wait()
    pltpu.make_async_copy(rows_hbm.at[pl.ds(0, G - 1)], rows_hbm.at[pl.ds(0, G - 1)], p_send).wait()


def exchange(keys8, rows):
    return pl.pallas_call(
        exchange_kernel,
        out_shape=(
            jax.ShapeDtypeStruct((G, 128), jnp.float32),
            jax.ShapeDtypeStruct((G, CAP, W), jnp.bfloat16),
        ),
        in_specs=[pl.BlockSpec(memory_space=pltpu.VMEM), pl.BlockSpec(memory_space=pl.ANY)],
        out_specs=(pl.BlockSpec(memory_space=pltpu.VMEM), pl.BlockSpec(memory_space=pl.ANY)),
        scratch_shapes=[
            pltpu.VMEM((N, W), jnp.bfloat16),
            pltpu.VMEM((N * T, 128), jnp.float32),
            pltpu.VMEM((16 * T, 128), jnp.float32),
            pltpu.VMEM((G, CAP, W), jnp.bfloat16),
            pltpu.VMEM((1, 128), jnp.float32),
            pltpu.VMEM((G, 128), jnp.float32),
            pltpu.VMEM((G, 128), jnp.float32),
            pltpu.VMEM((G, 128), jnp.float32),
            pltpu.VMEM((8, 128), jnp.float32),
            pltpu.VMEM((16, 128), jnp.int32),
            pltpu.VMEM((1, 128), jnp.int32),
            pltpu.SMEM((16, 128), jnp.int32),
            pltpu.SMEM((1, 128), jnp.int32),
        ] + [pltpu.SemaphoreType.DMA(())] * 9,
        compiler_params=pltpu.CompilerParams(
            collective_id=1, has_side_effects=True, vmem_limit_bytes=48 << 20),
    )(keys8, rows)


def order_kernel(rk_ref, rows_hbm, keys_out, pay_hbm, cnt_ref,
                 rows_b, rows_f, stage, outb, tab_v, tab_s, in_sem, tab_sem, out_sem):
    CH = 8
    per = OUT // CH
    loads = [
        pltpu.make_async_copy(rows_hbm.at[pl.ds(i * per, per), :], rows_b.at[pl.ds(i * per, per), :], in_sem.at[i])
        for i in range(CH)
    ]
    for l in loads:
        l.start()
    rk = rk_ref[...]
    kt = jnp.transpose(rk)[0:CAP, :]
    valid = (kt < PAD_KEY).astype(jnp.int32)
    n_valid = jnp.sum(jnp.sum(valid, axis=1, keepdims=True), axis=0, keepdims=True)
    cnt_ref[...] = jnp.broadcast_to(n_valid, (1, 128))
    rank_cols = []
    for t in range(CAP):
        col = rk[:, t : t + 1]
        acc = jnp.zeros((G, 128), jnp.int32)
        for u in range(CAP):
            acc = acc + (kt[u : u + 1, :] < col).astype(jnp.int32)
        rank_cols.append(jnp.sum(acc, axis=1, keepdims=True))
    for r in range(OUT // 128):
        want = lane_iota((G, 128)) + r * 128
        ks = jnp.zeros((G, 128), jnp.float32)
        ps = jnp.zeros((G, 128), jnp.int32)
        for t in range(CAP):
            hit = rank_cols[t] == want
            src = sub_iota((G, 128)) * CAP + t
            addr = (src >> 3) * (8 * T) + (src & 7)
            ks = ks + jnp.where(hit, rk[:, t : t + 1], 0.0)
            ps = ps + jnp.where(hit, addr, 0)
        live = (lane_iota((1, 128)) + r * 128) < n_valid
        keys_out[r : r + 1, :] = jnp.where(live, jnp.sum(ks, axis=0, keepdims=True), PAD_KEY)
        tab_v[r : r + 1, :] = jnp.where(live, jnp.sum(ps, axis=0, keepdims=True), OUT * T)
    tab = pltpu.make_async_copy(tab_v, tab_s, tab_sem)
    tab.start()
    rows_f[pl.ds(OUT * T, 8 * T), :] = jnp.zeros((8 * T, 128), jnp.float32)

    def widen(g, c):
        x = rows_b[pl.ds(pl.multiple_of(g * 16, 16), 16), :].astype(jnp.float32)
        base = pl.multiple_of(g * (16 * T), 16)
        for h in range(2):
            for t in range(T):
                rows_f[pl.ds(base + h * 8 * T + t * 8, 8), :] = x[h * 8 : h * 8 + 8, t * 128 : t * 128 + 128]
        return c

    for i in range(CH):
        loads[i].wait()
        lax.fori_loop(i * per // 16, (i + 1) * per // 16, widen, 0)
    tab.wait()

    def place(g, c):
        for t in range(16):
            pos = g * 16 + t
            addr = tab_s[pos >> 7, pos & 127]
            stage[pl.ds((t // 8) * 8 * T + (t % 8), T, stride=8), :] = rows_f[pl.ds(addr, T, stride=8), :]
        for q in range(T):
            block = jnp.concatenate(
                [stage[q * 8 : q * 8 + 8, :], stage[8 * T + q * 8 : 8 * T + q * 8 + 8, :]], axis=0)
            outb[pl.ds(pl.multiple_of(g * 16, 16), 16), q * 128 : q * 128 + 128] = block.astype(jnp.bfloat16)
        return c

    outs = []
    for i in range(CH):
        lax.fori_loop(i * per // 16, (i + 1) * per // 16, place, 0)
        o = pltpu.make_async_copy(outb.at[pl.ds(i * per, per), :], pay_hbm.at[pl.ds(i * per, per), :], out_sem.at[i])
        o.start()
        outs.append(o)
    for o in outs:
        o.wait()


def reorder(rk, rows):
    return pl.pallas_call(
        order_kernel,
        out_shape=(
            jax.ShapeDtypeStruct((OUT // 128, 128), jnp.float32),
            jax.ShapeDtypeStruct((OUT, W), jnp.bfloat16),
            jax.ShapeDtypeStruct((1, 128), jnp.int32),
        ),
        in_specs=[pl.BlockSpec(memory_space=pltpu.VMEM), pl.BlockSpec(memory_space=pl.ANY)],
        out_specs=(pl.BlockSpec(memory_space=pltpu.VMEM), pl.BlockSpec(memory_space=pl.ANY), pl.BlockSpec(memory_space=pltpu.VMEM)),
        scratch_shapes=[
            pltpu.VMEM((OUT, W), jnp.bfloat16),
            pltpu.VMEM((OUT * T + 8 * T, 128), jnp.float32),
            pltpu.VMEM((16 * T, 128), jnp.float32),
            pltpu.VMEM((OUT, W), jnp.bfloat16),
            pltpu.VMEM((16, 128), jnp.int32),
            pltpu.SMEM((16, 128), jnp.int32),
            pltpu.SemaphoreType.DMA((8,)),
            pltpu.SemaphoreType.DMA(()),
            pltpu.SemaphoreType.DMA((8,)),
        ],
        compiler_params=pltpu.CompilerParams(vmem_limit_bytes=48 << 20),
    )(rk, rows)


def solution(mesh):
    def local_part(keys_loc, rows_loc):
        rk, recv = exchange(keys_loc.reshape(8, 128), rows_loc)
        keys_out, rows_out, cnt = reorder(rk, recv.reshape(OUT, W))
        return keys_out.reshape(-1), rows_out, cnt[0, 0:1]

    row = P(("batch", "g"))
    mat = P(("batch", "g"), None)
    return jax.shard_map(local_part, mesh=mesh, in_specs=(row, mat), out_specs=(row, mat, row), check_vma=False)
```

time: 178 us -> 110 us (0.62); the launches traced: 176 us -> 110 us
  Pallas kernels: 0 us -> 107 us
  local copies, waits for them, and re-layouts: 51.6 us -> 2.18 us
  waiting for transfers between devices: 42.7 us -> 0 us
  blocking collectives: 38.7 us -> 0 us
  other arithmetic: 25.3 us -> 0 us
  starting transfers between devices: 16 us -> 0 us
    pallas_call x0 -> x2, Pallas kernels: none -> 107 us  [the longest x1 88.3 us: exchange(): pl.pallas_call(exchange_kernel, out_shape=(jax.ShapeDtypeStruct((G, 128),...]
    gather x17 -> x0, local copies, waits for them, and re-layouts: 50.4 us -> none  [the longest x1 12.9 us: local_part(): merged_rows = recv_rows.reshape(-1, width)[merge_order]]
    all_to_all x2 -> x0, waiting for transfers between devices: 42.7 us -> none  [the longest x1 42.7 us: local_part(): recv_rows = lax.all_to_all(send_rows, 'g', 0, 0, tiled=True)]
    all_gather x1 -> x0, blocking collectives: 38.7 us -> none  [local_part(): all_samples = jnp.sort(lax.all_gather(samples, 'g', tiled=True))]
    sort x3 -> x0, other arithmetic: 18.7 us -> none  [the longest x1 8.73 us: local_part(): all_samples = jnp.sort(lax.all_gather(samples, 'g', tiled=True))]
    all_to_all x2 -> x0, starting transfers between devices: 16 us -> none  [the longest x1 10.2 us: local_part(): recv_rows = lax.all_to_all(send_rows, 'g', 0, 0, tiled=True)]
    select_n x26 -> x0, other arithmetic: 4.75 us -> none  [the longest x1 3.63 us: local_part(): jnp.where(is_valid[:, :, None], rows_loc[sort_order[src_pos]], 0.0)]
    unnamed x2 -> x4, local copies, waits for them, and re-layouts: 0.01 us -> 2.18 us
  transfers between devices with their start and end apart: 2 -> 0, of which waited for: 1 -> 0; matrix products, arithmetic and copies ran while one was open for 17% -> 0% of each run, Pallas kernels for 0% -> 0%
where the time goes in v1:
time: 110 us
  Pallas kernels  107 us (97%)
  local copies, waits for them, and re-layouts  2.18 us (2%)
    pallas_call x1, Pallas kernels, exchange(): pl.pallas_call(exchange_kernel, out_shape=(jax.ShapeDtypeStruct((G, 128),...  88.3 us
    pallas_call x1, Pallas kernels, reorder(): pl.pallas_call(order_kernel, out_shape=(jax.ShapeDtypeStruct((OUT // 128,...  18.4 us

profile of v1, /device:TPU:1, one launch (start us, length us, event | category | flops | bytes accessed | tf_op | source)
XLA Modules:
  0.0 109.6 jit_solution(6090799686975230793)
XLA Ops:
  0.6 0.0 copy-start
  0.6 1.5 %copy-done = bf16[1024,896]{1,0:T(8,128)(2,1)S(1)} copy-done((bf16[1024,896]{1,0:T(8,128)(2,1)S(1)}, bf16[1024,896]{1,0:T(8,128)(2,1)}, u32[]{:S(2)}) %copy-start) | copy-done | bytes 1835032
  2.1 0.0 copy-start.1
  2.1 0.7 copy-done.1
  2.8 88.3 %shard_map.49 = (f32[128,128]{1,0:T(8,128)S(1)}, bf16[128,16,896]{2,1,0:T(8,128)(2,1)S(1)}) custom-call(f32[8,128]{1,0:T(8,128)S(1)} %bitcast.6, bf16[1024,896]{1,0:T(8,128)(2,1)S(1)} %copy-done), custom_call_target="tpu_custom_call" | custom-call | tf_op jit(solution)/shard_map/pallas_call | solution.py:195
  91.2 18.4 %shard_map.50 = (f32[16,128]{1,0:T(8,128)}, bf16[2048,896]{1,0:T(8,128)(2,1)}, s32[1,128]{1,0:T(1,128)}) custom-call(f32[128,128]{1,0:T(8,128)S(1)} %get-tuple-element.8.rk_ref, bf16[2048,896]{1,0:T(8,128)(2,1)S(1)} %bitcast.5), custom_call_target="tpu_custom_call" | custom-call | tf_op jit(solution)/shard_map/pallas_call | solution.py:297
Async XLA Ops:
  0.6 1.5 %copy-start = (bf16[1024,896]{1,0:T(8,128)(2,1)S(1)}, bf16[1024,896]{1,0:T(8,128)(2,1)}, u32[]{:S(2)}) copy-start(bf16[1024,896]{1,0:T(8,128)(2,1)} %pay_hbm.1) | copy-start | bytes 5505028
  2.1 0.7 copy-start.1

commit v2 on v1

v2 whole, which is shorter than its diff:
```python
import functools
import jax
import jax.numpy as jnp
from jax import lax
from jax.sharding import PartitionSpec as P
from jax.experimental import pallas as pl
from jax.experimental.pallas import tpu as pltpu

PAD_KEY = 128.0
G = 128
N = 1024
W = 896
T = 7
CAP = 16
OUT = 2048
STRIDE = 11
PER = 16
MESH = pl.DeviceIdType.MESH


def lane_iota(shape):
    return lax.broadcasted_iota(jnp.int32, shape, 1)


def sub_iota(shape):
    return lax.broadcasted_iota(jnp.int32, shape, 0)


def exchange_kernel(
    keys_hbm, pay_hbm, rows_f, tab_ref, keys_out, cnt_ref,
    keys_v, pay_b, pay_f, stage, sendbuf, recv, samp, runs, kbuf, rk, srt, tab_v, st_v, tab_s, st_s,
    key_sem, in_sem, tab_sem, self_sem, s_send, s_recv, k_send, k_recv, p_send, p_recv,
):
    me = lax.axis_index("g")
    barrier = pltpu.get_barrier_semaphore()

    def peer(k):
        return (me + k * STRIDE) & (G - 1)

    def greet(k, c):
        pl.semaphore_signal(barrier, inc=1, device_id={"g": peer(k)}, device_id_type=MESH)
        return c

    key_load = pltpu.make_async_copy(keys_hbm, keys_v, key_sem)
    key_load.start()
    load = pltpu.make_async_copy(pay_hbm, pay_b, in_sem)
    load.start()
    lax.fori_loop(1, G, greet, 0)
    key_load.wait()

    keys = keys_v[...]
    keys_t = jnp.transpose(keys)
    rank_cols = []
    for a in range(8):
        col = keys_t[:, a : a + 1]
        acc = jnp.zeros((G, 128), jnp.int32)
        for b in range(8):
            acc = acc + (keys[b : b + 1, :] < col).astype(jnp.int32)
        rank_cols.append(jnp.sum(acc, axis=1, keepdims=True))
    for r in range(8):
        want = lane_iota((G, 128)) * 8 + r
        ks = jnp.zeros((G, 128), jnp.float32)
        ps = jnp.zeros((G, 128), jnp.int32)
        for a in range(8):
            hit = rank_cols[a] == want
            src = sub_iota((G, 128)) + a * 128
            addr = (src >> 3) * (8 * T) + (src & 7)
            ks = ks + jnp.where(hit, keys_t[:, a : a + 1], 0.0)
            ps = ps + jnp.where(hit, addr, 0)
        row = jnp.sum(ks, axis=0, keepdims=True)
        srt[r : r + 1, :] = row
        if r == 0:
            samp[...] = row
        tab_v[r : r + 1, :] = jnp.sum(ps, axis=0, keepdims=True)
    tab_copy = pltpu.make_async_copy(tab_v, tab_s, tab_sem)
    tab_copy.start()

    pl.semaphore_wait(barrier, G - 1)

    def send_samples(k, c):
        pltpu.make_async_remote_copy(
            src_ref=samp, dst_ref=runs.at[pl.ds(me, 1), :], send_sem=s_send, recv_sem=s_recv,
            device_id={"g": peer(k)}, device_id_type=MESH,
        ).start()
        return c

    lax.fori_loop(1, G, send_samples, 0)

    load.wait()

    def widen_rows(g, c):
        x = pay_b[pl.ds(pl.multiple_of(g * 16, 16), 16), :].astype(jnp.float32)
        base = pl.multiple_of(g * (16 * T), 16)
        for h in range(2):
            for t in range(T):
                pay_f[pl.ds(base + h * 8 * T + t * 8, 8), :] = x[h * 8 : h * 8 + 8, t * 128 : t * 128 + 128]
        return c

    lax.fori_loop(0, N // 16, widen_rows, 0)
    tab_copy.wait()

    many = runs.at[pl.ds(0, G - 1), :]
    pltpu.make_async_copy(many, many, s_recv).wait()
    pltpu.make_async_copy(many, many, s_send).wait()
    runs[pl.ds(me, 1), :] = samp[...]

    def reach(q_col):
        q = jnp.broadcast_to(q_col, (G, 128))

        def step(i, acc):
            for u in range(8):
                acc = acc + (runs[pl.ds(i * 8 + u, 1), :] <= q).astype(jnp.int32)
            return acc

        return jnp.sum(lax.fori_loop(0, G // 8, step, jnp.zeros((G, 128), jnp.int32)), axis=1, keepdims=True)

    sorted8 = srt[...]
    sorted8_t = jnp.transpose(sorted8)
    lanes = lane_iota((G, 128))
    need_row = jnp.where(lanes == 0, 0, lanes * 128 + 65)
    below = (reach(sorted8_t[:, 0:1]) < need_row).astype(jnp.int32)
    n_row = jnp.sum(below, axis=0, keepdims=True)
    at = jnp.broadcast_to(jnp.maximum(n_row - 1, 0), (8, 128))
    near = jnp.take_along_axis(sorted8, at, axis=1)
    near_t = jnp.transpose(near)
    n_t = jnp.transpose(jnp.broadcast_to(n_row, (8, 128)))[:, 0:1]
    dests = lax.broadcasted_iota(jnp.int32, (G, 1), 0)
    need = jnp.where(dests == 0, 0, dests * 128 + 65)
    pos = jnp.zeros((G, 1), jnp.int32)
    for width in (4, 2, 1):
        q = jnp.zeros((G, 1), jnp.float32)
        for j in range(width, 8, 2 * width):
            q = jnp.where(pos + width == j, near_t[:, j : j + 1], q)
        pos = pos + jnp.where(reach(q) < need, width, 0)
    start_col = jnp.where(n_t > 0, (n_t - 1) * 8 + pos + 1, 0)
    start = jnp.transpose(jnp.broadcast_to(start_col, (G, 128)))[0:1, :]
    stop = jnp.where(lanes[0:1, :] == G - 1, N, pltpu.roll(start, G - 1, 1))
    st_v[...] = start
    st_copy = pltpu.make_async_copy(st_v, st_s, tab_sem)
    st_copy.start()

    stop_col = jnp.transpose(jnp.broadcast_to(stop, (8, 128)))[:, 0:1]
    tables = [jnp.broadcast_to(sorted8[b : b + 1, :], (8, 128)) for b in range(8)]
    for dg in range(16):
        first = start_col[dg * 8 : dg * 8 + 8, :]
        last = stop_col[dg * 8 : dg * 8 + 8, :]
        slot = lane_iota((8, 128))
        idx = first + slot
        pick = (idx >> 3) & 127
        part = idx & 7
        val = jnp.full((8, 128), PAD_KEY, jnp.float32)
        for b in range(8):
            val = jnp.where(part == b, jnp.take_along_axis(tables[b], pick, axis=1), val)
        kbuf[dg * 8 : dg * 8 + 8, :] = jnp.where((idx < last) & (slot < CAP), val, PAD_KEY)
    st_copy.wait()

    def build(d):
        first = st_s[0, d]
        for t in range(CAP):
            pos = jnp.minimum(first + t, N - 1)
            addr = tab_s[pos & 7, pos >> 3]
            stage[pl.ds((t // 8) * 8 * T + (t % 8), T, stride=8), :] = pay_f[pl.ds(addr, T, stride=8), :]
        for c in range(T):
            block = jnp.concatenate(
                [stage[c * 8 : c * 8 + 8, :], stage[8 * T + c * 8 : 8 * T + c * 8 + 8, :]], axis=0)
            sendbuf[d, :, c * 128 : c * 128 + 128] = block.astype(jnp.bfloat16)

    def send_block(k):
        p = peer(k)
        build(p)
        pltpu.make_async_remote_copy(
            src_ref=sendbuf.at[p], dst_ref=recv.at[me], send_sem=p_send, recv_sem=p_recv.at[k // PER],
            device_id={"g": p}, device_id_type=MESH,
        ).start()

    def send_keys(k):
        p = peer(k)
        pltpu.make_async_remote_copy(
            src_ref=kbuf.at[pl.ds(p, 1), :], dst_ref=rk.at[pl.ds(me, 1), :], send_sem=k_send, recv_sem=k_recv,
            device_id={"g": p}, device_id_type=MESH,
        ).start()

    def send_both(i, c):
        send_block(i + 1)
        for u in range(8):
            k = i * 8 + u + 1

            @pl.when(k < G)
            def _():
                send_keys(k)
        return c

    lax.fori_loop(0, G // 8, send_both, 0)

    def send_rows(k, c):
        send_block(k)
        return c

    lax.fori_loop(G // 8 + 1, G, send_rows, 0)
    build(me)
    own = pltpu.make_async_copy(sendbuf.at[me], recv.at[me], self_sem)
    own.start()

    many_k = rk.at[pl.ds(0, G - 1), :]
    pltpu.make_async_copy(many_k, many_k, k_recv).wait()
    pltpu.make_async_copy(many_k, many_k, k_send).wait()
    rk[pl.ds(me, 1), :] = kbuf[pl.ds(me, 1), :]
    got = rk[...]
    kt = jnp.transpose(got)[0:CAP, :]
    valid = (kt < PAD_KEY).astype(jnp.int32)
    n_valid = jnp.sum(jnp.sum(valid, axis=1, keepdims=True), axis=0, keepdims=True)
    cnt_ref[...] = jnp.broadcast_to(n_valid, (1, 128))
    cols = []
    for t in range(CAP):
        col = got[:, t : t + 1]
        acc = jnp.zeros((G, 128), jnp.int32)
        for u in range(CAP):
            acc = acc + (kt[u : u + 1, :] < col).astype(jnp.int32)
        cols.append(jnp.sum(acc, axis=1, keepdims=True))
    places = []
    for r in range(OUT // 128):
        want = lane_iota((G, 128)) + r * 128
        wish = lane_iota((G, 128)) * 16 + r
        ks = jnp.zeros((G, 128), jnp.float32)
        ps = jnp.zeros((G, 128), jnp.int32)
        for t in range(CAP):
            src = sub_iota((G, 128)) * CAP + t
            addr = (src >> 3) * (8 * T) + (src & 7)
            ks = ks + jnp.where(cols[t] == want, got[:, t : t + 1], 0.0)
            ps = ps + jnp.where(cols[t] == wish, addr, 0)
        live = want[0:1, :] < n_valid
        keys_out[r : r + 1, :] = jnp.where(live, jnp.sum(ks, axis=0, keepdims=True), PAD_KEY)
        places.append(jnp.where(wish[0:1, :] < n_valid, jnp.sum(ps, axis=0, keepdims=True), OUT * T))
    tab_ref[...] = jnp.transpose(jnp.concatenate(places, axis=0))
    rows_f[pl.ds(OUT * T, 8 * T), :] = jnp.zeros((8 * T, 128), jnp.float32)

    def widen_block(src):
        x = recv[src].astype(jnp.float32)
        base = pl.multiple_of(src * (16 * T), 16)
        for h in range(2):
            for t in range(T):
                rows_f[pl.ds(base + h * 8 * T + t * 8, 8), :] = x[h * 8 : h * 8 + 8, t * 128 : t * 128 + 128]

    own.wait()
    widen_block(me)
    for g in range(G // PER):
        n = PER - 1 if g == 0 else PER
        part = recv.at[pl.ds(0, n)]
        pltpu.make_async_copy(part, part, p_recv.at[g]).wait()

        def widen_from(k, c):
            widen_block((me - k * STRIDE) & (G - 1))
            return c

        lax.fori_loop(max(1, g * PER), (g + 1) * PER, widen_from, 0)
    sent = sendbuf.at[pl.ds(0, G - 1)]
    pltpu.make_async_copy(sent, sent, p_send).wait()


def exchange(keys8, rows):
    vmem = pl.BlockSpec(memory_space=pltpu.VMEM)
    hbm = pl.BlockSpec(memory_space=pltpu.HBM)
    return pl.pallas_call(
        exchange_kernel,
        out_shape=(
            jax.ShapeDtypeStruct(((OUT + 8) * T, 128), jnp.float32),
            jax.ShapeDtypeStruct((G, 16), jnp.int32),
            jax.ShapeDtypeStruct((OUT // 128, 128), jnp.float32),
            jax.ShapeDtypeStruct((1, 128), jnp.int32),
        ),
        in_specs=[hbm, hbm],
        out_specs=(vmem, vmem, vmem, vmem),
        scratch_shapes=[
            pltpu.VMEM((8, 128), jnp.float32),
            pltpu.VMEM((N, W), jnp.bfloat16),
            pltpu.VMEM((N * T, 128), jnp.float32),
            pltpu.VMEM((16 * T, 128), jnp.float32),
            pltpu.VMEM((G, CAP, W), jnp.bfloat16),
            pltpu.VMEM((G, CAP, W), jnp.bfloat16),
            pltpu.VMEM((1, 128), jnp.float32),
            pltpu.VMEM((G, 128), jnp.float32),
            pltpu.VMEM((G, 128), jnp.float32),
            pltpu.VMEM((G, 128), jnp.float32),
            pltpu.VMEM((8, 128), jnp.float32),
            pltpu.VMEM((8, 128), jnp.int32),
            pltpu.VMEM((1, 128), jnp.int32),
            pltpu.SMEM((8, 128), jnp.int32),
            pltpu.SMEM((1, 128), jnp.int32),
        ] + [pltpu.SemaphoreType.DMA(())] * 9 + [pltpu.SemaphoreType.DMA((G // PER,))],
        compiler_params=pltpu.CompilerParams(
            collective_id=1, has_side_effects=True, vmem_limit_bytes=40 << 20),
    )(keys8, rows)


def order_kernel(tab_s, cnt_s, rows_f, pay_hbm, stage, outb, zeros, out_sem):
    count = cnt_s[0, 0]
    rows = 128
    chunks = OUT // rows
    zeros[...] = jnp.zeros((rows, W), jnp.bfloat16)

    def store(i, src):
        return pltpu.make_async_copy(
            src, pay_hbm.at[pl.ds(pl.multiple_of(i * rows, rows), rows), :], out_sem.at[i])

    def place(g, c):
        for t in range(16):
            addr = tab_s[g, t]
            stage[pl.ds((t // 8) * 8 * T + (t % 8), T, stride=8), :] = rows_f[pl.ds(addr, T, stride=8), :]
        for q in range(T):
            block = jnp.concatenate(
                [stage[q * 8 : q * 8 + 8, :], stage[8 * T + q * 8 : 8 * T + q * 8 + 8, :]], axis=0)
            outb[pl.ds(pl.multiple_of(g * 16, 16), 16), q * 128 : q * 128 + 128] = block.astype(jnp.bfloat16)
        return c

    def empty(i, c):
        @pl.when(i * rows >= count)
        def _():
            store(i, zeros).start()
        return c

    def full(i, c):
        @pl.when(i * rows < count)
        def _():
            lax.fori_loop(i * (rows // 16), (i + 1) * (rows // 16), place, 0)
            store(i, outb.at[pl.ds(pl.multiple_of(i * rows, rows), rows), :]).start()
        return c

    def finish(i, c):
        store(i, zeros).wait()
        return c

    lax.fori_loop(0, chunks, empty, 0)
    lax.fori_loop(0, chunks, full, 0)
    lax.fori_loop(0, chunks, finish, 0)


def reorder(tab, cnt, rows_f):
    smem = pl.BlockSpec(memory_space=pltpu.SMEM)
    return pl.pallas_call(
        order_kernel,
        out_shape=jax.ShapeDtypeStruct((OUT, W), jnp.bfloat16),
        in_specs=[smem, smem, pl.BlockSpec(memory_space=pltpu.VMEM)],
        out_specs=pl.BlockSpec(memory_space=pltpu.HBM),
        scratch_shapes=[
            pltpu.VMEM((16 * T, 128), jnp.float32),
            pltpu.VMEM((OUT, W), jnp.bfloat16),
            pltpu.VMEM((128, W), jnp.bfloat16),
            pltpu.SemaphoreType.DMA((OUT // 128,)),
        ],
        compiler_params=pltpu.CompilerParams(vmem_limit_bytes=24 << 20),
    )(tab, cnt, rows_f)


def solution(mesh):
    def local_part(keys_loc, rows_loc):
        rows_f, tab, keys_out, cnt = exchange(pltpu.with_memory_space_constraint(keys_loc.reshape(8, 128), pltpu.HBM), pltpu.with_memory_space_constraint(rows_loc, pltpu.HBM))
        rows_out = reorder(tab, cnt, rows_f)
        return keys_out.reshape(-1), rows_out, cnt[0, 0:1]

    row = P(("batch", "g"))
    mat = P(("batch", "g"), None)
    return jax.shard_map(local_part, mesh=mesh, in_specs=(row, mat), out_specs=(row, mat, row), check_vma=False)
```

time: 110 us -> 82 us (0.75)
  Pallas kernels: 107 us -> 79.5 us
  local copies, waits for them, and re-layouts: 2.18 us -> 0.6 us
  between operations: 0.65 us -> 1.81 us
    pallas_call x2, Pallas kernels: 107 us -> 79.5 us  [the longest x1 74.6 us: exchange(): pl.pallas_call(exchange_kernel, out_shape=(jax.ShapeDtypeStruct(((OUT + 8...]
    unnamed x4 -> x1, local copies, waits for them, and re-layouts: 2.18 us -> 0.6 us
where the time goes in v2:
time: 82 us; the launch traced here: 81.9 us
  Pallas kernels  79.5 us (97%)
  between operations  1.81 us (2%)
    pallas_call x1, Pallas kernels, exchange(): pl.pallas_call(exchange_kernel, out_shape=(jax.ShapeDtypeStruct(((OUT + 8...  74.6 us
    pallas_call x1, Pallas kernels, reorder(): pl.pallas_call(order_kernel, out_shape=jax.ShapeDtypeStruct((OUT, W), jnp...  4.86 us

profile of v2, /device:TPU:1, one launch (start us, length us, event | category | flops | bytes accessed | tf_op | source)
XLA Modules:
  0.0 81.9 jit_solution(296439489519591722)
XLA Ops:
  0.6 74.6 %shard_map.49 = (f32[14392,128]{1,0:T(8,128)S(1)}, s32[128,16]{1,0:T(8,128)S(1)}, f32[16,128]{1,0:T(8,128)S(1)}, s32[1,128]{1,0:T(1,128)S(1)}) custom-call(f32[8,128]{1,0:T(8,128)} %bitcast.6, bf16[1024,896]{1,0:T(8,128)(2,1)} %pay_hbm.1), custom_call_target="tpu_custom_call" | custom-call | tf_op jit(solution)/shard_map/pallas_call | solution.py:263
  75.2 4.9 %shard_map.50 = bf16[2048,896]{1,0:T(8,128)(2,1)} custom-call(s32[128,16]{1,0:T(8,128)S(1)} %get-tuple-element.8.tab_s, s32[1,128]{1,0:T(1,128)S(1)} %get-tuple-element.9.cnt_s, f32[14392,128]{1,0:T(8,128)S(1)} %get-tuple-element.10.rows_f), custom_call_target="tpu_custom_call" | custom-call | tf_op jit(solution)/shard_map/pallas_call | solution.py:339
  80.1 0.6 copy.7

commit v3 on v2

--- a/solution.py
+++ b/solution.py
@@ -14,7 +14,10 @@
 CAP = 16
 OUT = 2048
 STRIDE = 11
-PER = 16
+CHIPS = G // 2
+HOP = 13
+PART = 8
+PER = 8
 MESH = pl.DeviceIdType.MESH
 
 
@@ -28,14 +31,24 @@
 
 def exchange_kernel(
     keys_hbm, pay_hbm, rows_f, tab_ref, keys_out, cnt_ref,
-    keys_v, pay_b, pay_f, stage, sendbuf, recv, samp, runs, kbuf, rk, srt, tab_v, st_v, tab_s, st_s,
-    key_sem, in_sem, tab_sem, self_sem, s_send, s_recv, k_send, k_recv, p_send, p_recv,
+    keys_v, pay_b, pay_f, stage, sendbuf, recv, extra, samp, runs, kbuf, rk, srt, tab_v, st_v, tab_s, st_s,
+    key_sem, in_sem, tab_sem, self_sem, s_send, s_recv, k_send, k_recv, p_send, f_send, p_recv, e_recv, f_recv,
 ):
     me = lax.axis_index("g")
     barrier = pltpu.get_barrier_semaphore()
 
     def peer(k):
         return (me + k * STRIDE) & (G - 1)
+
+    core = me & 1
+    chip = me // 2
+    mate = me + 1 - 2 * core
+
+    def ahead(k):
+        return (chip + k * HOP) & (CHIPS - 1)
+
+    def behind(k):
+        return (chip - k * HOP) & (CHIPS - 1)
 
     def greet(k, c):
         pl.semaphore_signal(barrier, inc=1, device_id={"g": peer(k)}, device_id_type=MESH)
@@ -135,7 +148,13 @@
     start_col = jnp.where(n_t > 0, (n_t - 1) * 8 + pos + 1, 0)
     start = jnp.transpose(jnp.broadcast_to(start_col, (G, 128)))[0:1, :]
     stop = jnp.where(lanes[0:1, :] == G - 1, N, pltpu.roll(start, G - 1, 1))
-    st_v[...] = start
+    over = jnp.maximum(stop - start - PART, 0)
+    odd = (lanes[0:1, :] & 1) == 1
+    shift = jnp.where(odd, pltpu.roll(over, 1, 1), 0)
+    full = jnp.where(odd & (over + shift > PART), 1, 0)
+    full = jnp.max(full, axis=1, keepdims=True).astype(jnp.float32)
+    shift_col = jnp.transpose(jnp.broadcast_to(shift, (8, 128)))[:, 0:1].astype(jnp.float32)
+    st_v[...] = jnp.concatenate([start, over, jnp.zeros((6, 128), jnp.int32)], axis=0)
     st_copy = pltpu.make_async_copy(st_v, st_s, tab_sem)
     st_copy.start()
 
@@ -151,27 +170,41 @@
         val = jnp.full((8, 128), PAD_KEY, jnp.float32)
         for b in range(8):
             val = jnp.where(part == b, jnp.take_along_axis(tables[b], pick, axis=1), val)
-        kbuf[dg * 8 : dg * 8 + 8, :] = jnp.where((idx < last) & (slot < CAP), val, PAD_KEY)
+        val = jnp.where((idx < last) & (slot < CAP), val, PAD_KEY)
+        val = jnp.where(slot == CAP, shift_col[dg * 8 : dg * 8 + 8, :], val)
+        kbuf[dg * 8 : dg * 8 + 8, :] = jnp.where(slot == CAP + 1, full, val)
     st_copy.wait()
 
-    def build(d):
-        first = st_s[0, d]
-        for t in range(CAP):
-            pos = jnp.minimum(first + t, N - 1)
-            addr = tab_s[pos & 7, pos >> 3]
-            stage[pl.ds((t // 8) * 8 * T + (t % 8), T, stride=8), :] = pay_f[pl.ds(addr, T, stride=8), :]
-        for c in range(T):
-            block = jnp.concatenate(
-                [stage[c * 8 : c * 8 + 8, :], stage[8 * T + c * 8 : 8 * T + c * 8 + 8, :]], axis=0)
-            sendbuf[d, :, c * 128 : c * 128 + 128] = block.astype(jnp.bfloat16)
+    def row_at(pos):
+        pos = jnp.minimum(pos, N - 1)
+        return pay_f[pl.ds(tab_s[pos & 7, pos >> 3], T, stride=8), :]
+
+    def build(j):
+        first = st_s[0, 2 * j]
+        second = st_s[0, 2 * j + 1]
+        split = st_s[1, 2 * j]
+        for t in range(PART):
+            stage[pl.ds(t, T, stride=8), :] = row_at(first + t)
+            stage[pl.ds(8 * T + t, T, stride=8), :] = row_at(second + t)
+            stage[pl.ds(16 * T + t, T, stride=8), :] = row_at(
+                jnp.where(t < split, first + PART + t, second + PART + t - split))
+        for h in range(3):
+            for c in range(T):
+                base = h * 8 * T + c * 8
+                sendbuf[j * 3 + h, :, c * 128 : c * 128 + 128] = stage[base : base + 8, :].astype(jnp.bfloat16)
+
+    def send_part(src, dst, to, sem):
+        pltpu.make_async_remote_copy(
+            src_ref=src, dst_ref=dst.at[me], send_sem=p_send, recv_sem=sem,
+            device_id={"g": to}, device_id_type=MESH,
+        ).start()
 
     def send_block(k):
-        p = peer(k)
-        build(p)
-        pltpu.make_async_remote_copy(
-            src_ref=sendbuf.at[p], dst_ref=recv.at[me], send_sem=p_send, recv_sem=p_recv.at[k // PER],
-            device_id={"g": p}, device_id_type=MESH,
-        ).start()
+        j = ahead(k)
+        build(j)
+        send_part(sendbuf.at[j * 3 + 2], extra, 2 * j + core, e_recv.at[k])
+        send_part(sendbuf.at[j * 3], recv, 2 * j, p_recv.at[k // PER])
+        send_part(sendbuf.at[j * 3 + 1], recv, 2 * j + 1, p_recv.at[k // PER])
 
     def send_keys(k):
         p = peer(k)
@@ -196,10 +229,14 @@
         send_block(k)
         return c
 
-    lax.fori_loop(G // 8 + 1, G, send_rows, 0)
-    build(me)
-    own = pltpu.make_async_copy(sendbuf.at[me], recv.at[me], self_sem)
+    lax.fori_loop(G // 8 + 1, CHIPS, send_rows, 0)
+    build(chip)
+    send_part(sendbuf.at[chip * 3 + 1 - core], recv, mate, p_recv.at[0])
+    send_part(sendbuf.at[chip * 3 + 2], extra, mate, f_recv.at[0])
+    own = pltpu.make_async_copy(sendbuf.at[chip * 3 + core], recv.at[me], self_sem)
     own.start()
+    own_extra = pltpu.make_async_copy(sendbuf.at[chip * 3 + 2], extra.at[me], key_sem)
+    own_extra.start()
 
     many_k = rk.at[pl.ds(0, G - 1), :]
     pltpu.make_async_copy(many_k, many_k, k_recv).wait()
@@ -209,7 +246,9 @@
     kt = jnp.transpose(got)[0:CAP, :]
     valid = (kt < PAD_KEY).astype(jnp.int32)
     n_valid = jnp.sum(jnp.sum(valid, axis=1, keepdims=True), axis=0, keepdims=True)
-    cnt_ref[...] = jnp.broadcast_to(n_valid, (1, 128))
+    any_full = jnp.max(got[:, CAP + 1 : CAP + 2], axis=0, keepdims=True).astype(jnp.int32)
+    cnt_ref[...] = jnp.where(lanes[0:1, :] == 0, n_valid, any_full)
+    skip = got[:, CAP : CAP + 1].astype(jnp.int32)
     cols = []
     for t in range(CAP):
         col = got[:, t : t + 1]
@@ -224,8 +263,10 @@
         ks = jnp.zeros((G, 128), jnp.float32)
         ps = jnp.zeros((G, 128), jnp.int32)
         for t in range(CAP):
-            src = sub_iota((G, 128)) * CAP + t
-            addr = (src >> 3) * (8 * T) + (src & 7)
+            if t < PART:
+                addr = sub_iota((G, 1)) * (8 * T) + t
+            else:
+                addr = (sub_iota((G, 1)) + G) * (8 * T) + jnp.minimum(skip + (t - PART), PART - 1)
             ks = ks + jnp.where(cols[t] == want, got[:, t : t + 1], 0.0)
             ps = ps + jnp.where(cols[t] == wish, addr, 0)
         live = want[0:1, :] < n_valid
@@ -234,27 +275,58 @@
     tab_ref[...] = jnp.transpose(jnp.concatenate(places, axis=0))
     rows_f[pl.ds(OUT * T, 8 * T), :] = jnp.zeros((8 * T, 128), jnp.float32)
 
-    def widen_block(src):
-        x = recv[src].astype(jnp.float32)
-        base = pl.multiple_of(src * (16 * T), 16)
-        for h in range(2):
-            for t in range(T):
-                rows_f[pl.ds(base + h * 8 * T + t * 8, 8), :] = x[h * 8 : h * 8 + 8, t * 128 : t * 128 + 128]
+    def widen(part, src, first):
+        x = part[src].astype(jnp.float32)
+        base = pl.multiple_of((first + src) * (8 * T), 8)
+        for t in range(T):
+            rows_f[pl.ds(base + t * 8, 8), :] = x[:, t * 128 : t * 128 + 128]
 
     own.wait()
-    widen_block(me)
-    for g in range(G // PER):
-        n = PER - 1 if g == 0 else PER
-        part = recv.at[pl.ds(0, n)]
-        pltpu.make_async_copy(part, part, p_recv.at[g]).wait()
-
-        def widen_from(k, c):
-            widen_block((me - k * STRIDE) & (G - 1))
-            return c
-
-        lax.fori_loop(max(1, g * PER), (g + 1) * PER, widen_from, 0)
-    sent = sendbuf.at[pl.ds(0, G - 1)]
+    own_extra.wait()
+    widen(recv, me, 0)
+    widen(extra, me, G)
+    one = extra.at[0]
+
+    def forward(k, c):
+        pltpu.make_async_copy(one, one, e_recv.at[k]).wait()
+        src = 2 * behind(k) + core
+        pltpu.make_async_remote_copy(
+            src_ref=extra.at[src], dst_ref=extra.at[src], send_sem=f_send, recv_sem=f_recv.at[k // PER],
+            device_id={"g": mate}, device_id_type=MESH,
+        ).start()
+        return c
+
+    def widen_direct(k, c):
+        j = behind(k)
+        widen(recv, 2 * j, 0)
+        widen(recv, 2 * j + 1, 0)
+        widen(extra, 2 * j + core, G)
+        return c
+
+    def widen_forwarded(k, c):
+        widen(extra, 2 * behind(k) + 1 - core, G)
+        return c
+
+    for g in range(CHIPS // PER):
+        lo = max(1, g * PER)
+        hi = (g + 1) * PER
+        lax.fori_loop(lo, hi, forward, 0)
+        got_part = recv.at[pl.ds(0, 2 * PER - 1 if g == 0 else 2 * PER)]
+        pltpu.make_async_copy(got_part, got_part, p_recv.at[g]).wait()
+        if g == 0:
+            widen(recv, mate, 0)
+        lax.fori_loop(lo, hi, widen_direct, 0)
+        if g > 0:
+            fw = extra.at[pl.ds(0, PER)]
+            pltpu.make_async_copy(fw, fw, f_recv.at[g - 1]).wait()
+            lax.fori_loop((g - 1) * PER, g * PER, widen_forwarded, 0)
+    fw = extra.at[pl.ds(0, PER)]
+    pltpu.make_async_copy(fw, fw, f_recv.at[CHIPS // PER - 1]).wait()
+    lax.fori_loop(CHIPS - PER, CHIPS, widen_forwarded, 0)
+    sent = sendbuf.at[pl.ds(0, 3 * (CHIPS - 1) + 2)]
     pltpu.make_async_copy(sent, sent, p_send).wait()
+    passed = extra.at[pl.ds(0, CHIPS - 1)]
+    pltpu.make_async_copy(passed, passed, f_send).wait()
 
 
 def exchange(keys8, rows):
@@ -274,19 +346,24 @@
             pltpu.VMEM((8, 128), jnp.float32),
             pltpu.VMEM((N, W), jnp.bfloat16),
             pltpu.VMEM((N * T, 128), jnp.float32),
-            pltpu.VMEM((16 * T, 128), jnp.float32),
-            pltpu.VMEM((G, CAP, W), jnp.bfloat16),
-            pltpu.VMEM((G, CAP, W), jnp.bfloat16),
+            pltpu.VMEM((24 * T, 128), jnp.float32),
+            pltpu.VMEM((3 * CHIPS, PART, W), jnp.bfloat16),
+            pltpu.VMEM((G, PART, W), jnp.bfloat16),
+            pltpu.VMEM((G, PART, W), jnp.bfloat16),
             pltpu.VMEM((1, 128), jnp.float32),
             pltpu.VMEM((G, 128), jnp.float32),
             pltpu.VMEM((G, 128), jnp.float32),
             pltpu.VMEM((G, 128), jnp.float32),
             pltpu.VMEM((8, 128), jnp.float32),
             pltpu.VMEM((8, 128), jnp.int32),
-            pltpu.VMEM((1, 128), jnp.int32),
+            pltpu.VMEM((8, 128), jnp.int32),
             pltpu.SMEM((8, 128), jnp.int32),
-            pltpu.SMEM((1, 128), jnp.int32),
-        ] + [pltpu.SemaphoreType.DMA(())] * 9 + [pltpu.SemaphoreType.DMA((G // PER,))],
+            pltpu.SMEM((8, 128), jnp.int32),
+        ] + [pltpu.SemaphoreType.DMA(())] * 10 + [
+            pltpu.SemaphoreType.DMA((CHIPS // PER,)),
+            pltpu.SemaphoreType.DMA((CHIPS,)),
+            pltpu.SemaphoreType.DMA((CHIPS // PER,)),
+        ],
         compiler_params=pltpu.CompilerParams(
             collective_id=1, has_side_effects=True, vmem_limit_bytes=40 << 20),
     )(keys8, rows)
@@ -351,11 +428,40 @@
     )(tab, cnt, rows_f)
 
 
+def plain_sort(keys_loc, rows_loc):
+    sorted_keys, sort_order = lax.sort((keys_loc, lax.iota(jnp.int32, N)), num_keys=1)
+    samples = sorted_keys[:: N // G]
+    all_samples = jnp.sort(lax.all_gather(samples, "g", tiled=True))
+    splitters = all_samples[G + G // 2 :: G]
+    edges = jnp.searchsorted(sorted_keys, splitters, side="left").astype(jnp.int32)
+    starts = jnp.concatenate([jnp.zeros((1,), jnp.int32), edges])
+    stops = jnp.concatenate([edges, jnp.full((1,), N, jnp.int32)])
+    src_pos = starts[:, None] + lax.iota(jnp.int32, CAP)[None, :]
+    is_valid = src_pos < stops[:, None]
+    src_pos = jnp.minimum(src_pos, N - 1)
+    send_keys = jnp.where(is_valid, sorted_keys[src_pos], PAD_KEY)
+    send_rows = jnp.where(is_valid[:, :, None], rows_loc[sort_order[src_pos]], 0.0)
+    recv_keys = lax.all_to_all(send_keys, "g", 0, 0, tiled=True)
+    recv_rows = lax.all_to_all(send_rows, "g", 0, 0, tiled=True)
+    flat_keys = recv_keys.reshape(-1)
+    merged_keys, merge_order = lax.sort((flat_keys, lax.iota(jnp.int32, OUT)), num_keys=1)
+    return merged_keys, recv_rows.reshape(-1, W)[merge_order]
+
+
 def solution(mesh):
     def local_part(keys_loc, rows_loc):
-        rows_f, tab, keys_out, cnt = exchange(pltpu.with_memory_space_constraint(keys_loc.reshape(8, 128), pltpu.HBM), pltpu.with_memory_space_constraint(rows_loc, pltpu.HBM))
+        rows_f, tab, keys_out, cnt = exchange(
+            pltpu.with_memory_space_constraint(keys_loc.reshape(8, 128), pltpu.HBM),
+            pltpu.with_memory_space_constraint(rows_loc, pltpu.HBM))
         rows_out = reorder(tab, cnt, rows_f)
-        return keys_out.reshape(-1), rows_out, cnt[0, 0:1]
+
+        def redo(state):
+            keys_all, rows_all = plain_sort(keys_loc, rows_loc)
+            return jnp.int32(0), keys_all, rows_all
+
+        _, keys_sorted, rows_sorted = lax.while_loop(
+            lambda state: state[0] > 0, redo, (cnt[0, 1], keys_out.reshape(-1), rows_out))
+        return keys_sorted, rows_sorted, cnt[0, 0:1]
 
     row = P(("batch", "g"))
     mat = P(("batch", "g"), None)

time: 82 us -> 75.7 us (0.923)
  Pallas kernels: 79.5 us -> 72.1 us
  local copies, waits for them, and re-layouts: 0.6 us -> 1.89 us
  between operations: 1.81 us -> 0.67 us
  loops' own time: 0 us -> 0.87 us
    pallas_call x1, Pallas kernels: 74.6 us -> 67.2 us  [exchange(): pl.pallas_call(exchange_kernel, out_shape=(jax.ShapeDtypeStruct(((OUT + 8...]
    another operation x0 -> x1, loops' own time: none -> 0.87 us  [local_part(): lax.while_loop(lambda state: state[0] > 0, redo, (cnt[0, 1], keys_out.res...]
where the time goes in v3:
time: 75.7 us; the launch traced here: 75.5 us
  Pallas kernels  72.1 us (95%)
  local copies, waits for them, and re-layouts  1.89 us (2%)
  loops' own time  0.87 us (1%)
    pallas_call x1, Pallas kernels, exchange(): pl.pallas_call(exchange_kernel, out_shape=(jax.ShapeDtypeStruct(((OUT + 8...  67.2 us
    pallas_call x1, Pallas kernels, reorder(): pl.pallas_call(order_kernel, out_shape=jax.ShapeDtypeStruct((OUT, W), jnp...  4.86 us

profile of v3, /device:TPU:1, one launch (start us, length us, event | category | flops | bytes accessed | tf_op | source)
XLA Modules:
  0.0 75.5 jit_solution(15546421071549520799)
XLA Ops:
  0.6 67.2 %shard_map.49 = (f32[14392,128]{1,0:T(8,128)S(1)}, s32[128,16]{1,0:T(8,128)S(1)}, f32[16,128]{1,0:T(8,128)}, s32[1,128]{1,0:T(1,128)S(1)}) custom-call(f32[8,128]{1,0:T(8,128)} %bitcast.15, bf16[1024,896]{1,0:T(8,128)(2,1)} %pay_hbm.1), custom_call_target="tpu_custom_call" | custom-call | tf_op jit(solution)/shard_map/pallas_call | solution.py:335
  67.9 0.0 copy-start
  67.9 0.0 copy-start.1
  67.9 4.9 %shard_map.50 = bf16[2048,896]{1,0:T(8,128)(2,1)} custom-call(s32[128,16]{1,0:T(8,128)S(1)} %get-tuple-element.111.tab_s, s32[1,128]{1,0:T(1,128)S(1)} %get-tuple-element.109.cnt_s, f32[14392,128]{1,0:T(8,128)S(1)} %get-tuple-element.112.rows_f), custom_call_target="tpu_custom_call" | custom-call | tf_op jit(solution)/shard_map/pallas_call | solution.py:416
  72.8 0.6 fusion.8
  73.3 0.0 copy-done
  73.3 0.0 copy-done.1
  73.3 0.9 %while.33 = (s32[]{:T(128)}, f32[2048]{0:T(1024)}, bf16[2048,896]{1,0:T(8,128)(2,1)}, f32[1024]{0:T(1024)S(1)}, bf16[1024,896]{1,0:T(8,128)(2,1)S(1)}) while((s32[]{:T(128)}, f32[2048]{0:T(1024)}, bf16[2048,896]{1,0:T(8,128)(2,1)}, f32[1024]{0:T(1024)S(1)}, bf16[1024,896]{1,0:T(8,128)(2,1)S(1)}) %tuple.56), condition=%region_6.7_spmd, body=%region_0.6_spmd | while | flops 2141794 | bytes 33904364 | solution.py:462
  74.2 1.3 %copy.27 = f32[2048]{0:T(1024)} copy(f32[2048]{0:T(1024)} %get-tuple-element.255) | data formatting | bytes 16384
Async XLA Ops:
  67.9 5.5 %copy-start = (bf16[1024,896]{1,0:T(8,128)(2,1)S(1)}, bf16[1024,896]{1,0:T(8,128)(2,1)}, u32[]{:S(2)}) copy-start(bf16[1024,896]{1,0:T(8,128)(2,1)} %pay_hbm.1) | copy-start | bytes 5505028
  67.9 5.5 %copy-start.1 = (f32[1024]{0:T(1024)S(1)}, f32[1024]{0:T(1024)}, u32[]{:S(2)}) copy-start(f32[1024]{0:T(1024)} %param.6) | copy-start | bytes 12292

commit v4 on v3

--- a/solution.py
+++ b/solution.py
@@ -15,8 +15,9 @@
 OUT = 2048
 STRIDE = 11
 CHIPS = G // 2
-HOP = 13
+HOP = 29
 PART = 8
+LAG = 21
 PER = 8
 MESH = pl.DeviceIdType.MESH
 
@@ -70,24 +71,22 @@
         for b in range(8):
             acc = acc + (keys[b : b + 1, :] < col).astype(jnp.int32)
         rank_cols.append(jnp.sum(acc, axis=1, keepdims=True))
-    for r in range(8):
+    def sort_row(r):
         want = lane_iota((G, 128)) * 8 + r
         ks = jnp.zeros((G, 128), jnp.float32)
         ps = jnp.zeros((G, 128), jnp.int32)
         for a in range(8):
             hit = rank_cols[a] == want
-            src = sub_iota((G, 128)) + a * 128
+            src = sub_iota((G, 1)) + a * 128
             addr = (src >> 3) * (8 * T) + (src & 7)
             ks = ks + jnp.where(hit, keys_t[:, a : a + 1], 0.0)
             ps = ps + jnp.where(hit, addr, 0)
         row = jnp.sum(ks, axis=0, keepdims=True)
         srt[r : r + 1, :] = row
-        if r == 0:
-            samp[...] = row
         tab_v[r : r + 1, :] = jnp.sum(ps, axis=0, keepdims=True)
-    tab_copy = pltpu.make_async_copy(tab_v, tab_s, tab_sem)
-    tab_copy.start()
-
+        return row
+
+    samp[...] = sort_row(0)
     pl.semaphore_wait(barrier, G - 1)
 
     def send_samples(k, c):
@@ -99,6 +98,10 @@
 
     lax.fori_loop(1, G, send_samples, 0)
 
+    for r in range(1, 8):
+        sort_row(r)
+    tab_copy = pltpu.make_async_copy(tab_v, tab_s, tab_sem)
+    tab_copy.start()
     load.wait()
 
     def widen_rows(g, c):
@@ -158,6 +161,77 @@
     st_copy = pltpu.make_async_copy(st_v, st_s, tab_sem)
     st_copy.start()
 
+    st_copy.wait()
+
+    def row_at(pos):
+        pos = jnp.minimum(pos, N - 1)
+        return pay_f[pl.ds(tab_s[pos & 7, pos >> 3], T, stride=8), :]
+
+    def build(j):
+        first = st_s[0, 2 * j]
+        second = st_s[0, 2 * j + 1]
+        split = st_s[1, 2 * j]
+        for t in range(PART):
+            stage[pl.ds(t, T, stride=8), :] = row_at(first + t)
+            stage[pl.ds(8 * T + t, T, stride=8), :] = row_at(second + t)
+            stage[pl.ds(16 * T + t, T, stride=8), :] = row_at(
+                jnp.where(t < split, first + PART + t, second + PART + t - split))
+        for h in range(3):
+            for c in range(T):
+                base = h * 8 * T + c * 8
+                sendbuf[j * 3 + h, :, c * 128 : c * 128 + 128] = stage[base : base + 8, :].astype(jnp.bfloat16)
+
+    def send_part(src, dst, to, sem):
+        pltpu.make_async_remote_copy(
+            src_ref=src, dst_ref=dst.at[me], send_sem=p_send, recv_sem=sem,
+            device_id={"g": to}, device_id_type=MESH,
+        ).start()
+
+    def send_c(k):
+        j = ahead(k)
+        build(j)
+        send_part(sendbuf.at[j * 3 + 2], extra, 2 * j + core, e_recv.at[k])
+
+    def send_a(k):
+        j = ahead(k)
+        send_part(sendbuf.at[j * 3], recv, 2 * j, p_recv.at[k // PER])
+
+    def send_b(k):
+        j = ahead(k)
+        send_part(sendbuf.at[j * 3 + 1], recv, 2 * j + 1, p_recv.at[k // PER])
+
+    def send_keys(k):
+        p = peer(k)
+        pltpu.make_async_remote_copy(
+            src_ref=kbuf.at[pl.ds(p, 1), :], dst_ref=rk.at[pl.ds(me, 1), :], send_sem=k_send, recv_sem=k_recv,
+            device_id={"g": p}, device_id_type=MESH,
+        ).start()
+
+    def key_steps(k, c):
+        send_c(k)
+        send_a(k - LAG)
+        for u in range(8):
+            i = (k - LAG) * 8 + u - 7
+
+            @pl.when(i < G)
+            def _():
+                send_keys(i)
+        return c
+
+    def steps(lo, hi, what):
+        def step(k, c):
+            if "c" in what:
+                send_c(k)
+            if "a" in what:
+                send_a(k - LAG)
+            if "b" in what:
+                send_b(k - 2 * LAG)
+            return c
+
+        lax.fori_loop(lo, hi, step, 0)
+
+    steps(1, LAG + 1, "c")
+
     stop_col = jnp.transpose(jnp.broadcast_to(stop, (8, 128)))[:, 0:1]
     tables = [jnp.broadcast_to(sorted8[b : b + 1, :], (8, 128)) for b in range(8)]
     for dg in range(16):
@@ -173,63 +247,12 @@
         val = jnp.where((idx < last) & (slot < CAP), val, PAD_KEY)
         val = jnp.where(slot == CAP, shift_col[dg * 8 : dg * 8 + 8, :], val)
         kbuf[dg * 8 : dg * 8 + 8, :] = jnp.where(slot == CAP + 1, full, val)
-    st_copy.wait()
-
-    def row_at(pos):
-        pos = jnp.minimum(pos, N - 1)
-        return pay_f[pl.ds(tab_s[pos & 7, pos >> 3], T, stride=8), :]
-
-    def build(j):
-        first = st_s[0, 2 * j]
-        second = st_s[0, 2 * j + 1]
-        split = st_s[1, 2 * j]
-        for t in range(PART):
-            stage[pl.ds(t, T, stride=8), :] = row_at(first + t)
-            stage[pl.ds(8 * T + t, T, stride=8), :] = row_at(second + t)
-            stage[pl.ds(16 * T + t, T, stride=8), :] = row_at(
-                jnp.where(t < split, first + PART + t, second + PART + t - split))
-        for h in range(3):
-            for c in range(T):
-                base = h * 8 * T + c * 8
-                sendbuf[j * 3 + h, :, c * 128 : c * 128 + 128] = stage[base : base + 8, :].astype(jnp.bfloat16)
-
-    def send_part(src, dst, to, sem):
-        pltpu.make_async_remote_copy(
-            src_ref=src, dst_ref=dst.at[me], send_sem=p_send, recv_sem=sem,
-            device_id={"g": to}, device_id_type=MESH,
-        ).start()
-
-    def send_block(k):
-        j = ahead(k)
-        build(j)
-        send_part(sendbuf.at[j * 3 + 2], extra, 2 * j + core, e_recv.at[k])
-        send_part(sendbuf.at[j * 3], recv, 2 * j, p_recv.at[k // PER])
-        send_part(sendbuf.at[j * 3 + 1], recv, 2 * j + 1, p_recv.at[k // PER])
-
-    def send_keys(k):
-        p = peer(k)
-        pltpu.make_async_remote_copy(
-            src_ref=kbuf.at[pl.ds(p, 1), :], dst_ref=rk.at[pl.ds(me, 1), :], send_sem=k_send, recv_sem=k_recv,
-            device_id={"g": p}, device_id_type=MESH,
-        ).start()
-
-    def send_both(i, c):
-        send_block(i + 1)
-        for u in range(8):
-            k = i * 8 + u + 1
-
-            @pl.when(k < G)
-            def _():
-                send_keys(k)
-        return c
-
-    lax.fori_loop(0, G // 8, send_both, 0)
-
-    def send_rows(k, c):
-        send_block(k)
-        return c
-
-    lax.fori_loop(G // 8 + 1, CHIPS, send_rows, 0)
+
+    lax.fori_loop(LAG + 1, LAG + 1 + G // 8, key_steps, 0)
+    steps(LAG + 1 + G // 8, 2 * LAG + 1, "ca")
+    steps(2 * LAG + 1, CHIPS, "cab")
+    steps(CHIPS, CHIPS + LAG, "ab")
+    steps(CHIPS + LAG, CHIPS + 2 * LAG, "b")
     build(chip)
     send_part(sendbuf.at[chip * 3 + 1 - core], recv, mate, p_recv.at[0])
     send_part(sendbuf.at[chip * 3 + 2], extra, mate, f_recv.at[0])
@@ -369,8 +392,16 @@
     )(keys8, rows)
 
 
-def order_kernel(tab_s, cnt_s, rows_f, pay_hbm, stage, outb, zeros, out_sem):
+def order_kernel(tab_s, cnt_s, rows_f, keys_v, pay_hbm, keys_hbm, cnt_hbm, flag_hbm, stage, outb, zeros, cnt_v, flag_v, out_sem, key_sem, cnt_sem, flag_sem):
     count = cnt_s[0, 0]
+    cnt_v[0] = count
+    flag_v[0] = cnt_s[0, 1]
+    cnt_store = pltpu.make_async_copy(cnt_v, cnt_hbm, cnt_sem)
+    cnt_store.start()
+    flag_store = pltpu.make_async_copy(flag_v, flag_hbm, flag_sem)
+    flag_store.start()
+    keys_store = pltpu.make_async_copy(keys_v, keys_hbm, key_sem)
+    keys_store.start()
     rows = 128
     chunks = OUT // rows
     zeros[...] = jnp.zeros((rows, W), jnp.bfloat16)
@@ -408,24 +439,36 @@
 
     lax.fori_loop(0, chunks, empty, 0)
     lax.fori_loop(0, chunks, full, 0)
+    keys_store.wait()
+    cnt_store.wait()
+    flag_store.wait()
     lax.fori_loop(0, chunks, finish, 0)
 
 
-def reorder(tab, cnt, rows_f):
+def reorder(tab, cnt, rows_f, keys):
     smem = pl.BlockSpec(memory_space=pltpu.SMEM)
+    vmem = pl.BlockSpec(memory_space=pltpu.VMEM)
+    hbm = pl.BlockSpec(memory_space=pltpu.HBM)
     return pl.pallas_call(
         order_kernel,
-        out_shape=jax.ShapeDtypeStruct((OUT, W), jnp.bfloat16),
-        in_specs=[smem, smem, pl.BlockSpec(memory_space=pltpu.VMEM)],
-        out_specs=pl.BlockSpec(memory_space=pltpu.HBM),
+        out_shape=(
+            jax.ShapeDtypeStruct((OUT, W), jnp.bfloat16),
+            jax.ShapeDtypeStruct((OUT // 128, 128), jnp.float32),
+            jax.ShapeDtypeStruct((1,), jnp.int32),
+            jax.ShapeDtypeStruct((1,), jnp.int32),
+        ),
+        in_specs=[smem, smem, vmem, vmem],
+        out_specs=(hbm, hbm, hbm, hbm),
         scratch_shapes=[
             pltpu.VMEM((16 * T, 128), jnp.float32),
             pltpu.VMEM((OUT, W), jnp.bfloat16),
             pltpu.VMEM((128, W), jnp.bfloat16),
+            pltpu.SMEM((1,), jnp.int32),
+            pltpu.SMEM((1,), jnp.int32),
             pltpu.SemaphoreType.DMA((OUT // 128,)),
-        ],
+        ] + [pltpu.SemaphoreType.DMA(())] * 3,
         compiler_params=pltpu.CompilerParams(vmem_limit_bytes=24 << 20),
-    )(tab, cnt, rows_f)
+    )(tab, cnt, rows_f, keys)
 
 
 def plain_sort(keys_loc, rows_loc):
@@ -453,15 +496,15 @@
         rows_f, tab, keys_out, cnt = exchange(
             pltpu.with_memory_space_constraint(keys_loc.reshape(8, 128), pltpu.HBM),
             pltpu.with_memory_space_constraint(rows_loc, pltpu.HBM))
-        rows_out = reorder(tab, cnt, rows_f)
+        rows_out, keys_out, count, flag = reorder(tab, cnt, rows_f, keys_out)
 
         def redo(state):
             keys_all, rows_all = plain_sort(keys_loc, rows_loc)
             return jnp.int32(0), keys_all, rows_all
 
         _, keys_sorted, rows_sorted = lax.while_loop(
-            lambda state: state[0] > 0, redo, (cnt[0, 1], keys_out.reshape(-1), rows_out))
-        return keys_sorted, rows_sorted, cnt[0, 0:1]
+            lambda state: state[0] > 0, redo, (flag.reshape(()), keys_out.reshape(-1), rows_out))
+        return keys_sorted, rows_sorted, count
 
     row = P(("batch", "g"))
     mat = P(("batch", "g"), None)

time: 75.7 us -> 69 us (0.911)
  Pallas kernels: 72.1 us -> 67.2 us
  local copies, waits for them, and re-layouts: 1.89 us -> 0.01 us
    pallas_call x1, Pallas kernels: 67.2 us -> 62.3 us  [exchange(): pl.pallas_call(exchange_kernel, out_shape=(jax.ShapeDtypeStruct(((OUT + 8...]
    unnamed x5 -> x4, local copies, waits for them, and re-layouts: 1.31 us -> 0.01 us
where the time goes in v4:
time: 69 us; the launch traced here: 68.9 us
  Pallas kernels  67.2 us (97%)
  between operations  0.86 us (1%)
  loops' own time  0.78 us (1%)
    pallas_call x1, Pallas kernels, exchange(): pl.pallas_call(exchange_kernel, out_shape=(jax.ShapeDtypeStruct(((OUT + 8...  62.3 us
    pallas_call x1, Pallas kernels, reorder(): pl.pallas_call(order_kernel, out_shape=(jax.ShapeDtypeStruct((OUT, W), jn...  4.89 us

profile of v4, /device:TPU:1, one launch (start us, length us, event | category | flops | bytes accessed | tf_op | source)
XLA Modules:
  0.0 68.9 jit_solution(10074309523374145744)
XLA Ops:
  0.6 62.3 %shard_map.49 = (f32[14392,128]{1,0:T(8,128)S(1)}, s32[128,16]{1,0:T(8,128)S(1)}, f32[16,128]{1,0:T(8,128)S(1)}, s32[1,128]{1,0:T(1,128)S(1)}) custom-call(f32[8,128]{1,0:T(8,128)} %bitcast.14, bf16[1024,896]{1,0:T(8,128)(2,1)} %pay_hbm.1), custom_call_target="tpu_custom_call" | custom-call | tf_op jit(solution)/shard_map/pallas_call | solution.py:358
  63.0 0.0 copy-start
  63.0 0.0 copy-start.1
  63.0 4.9 %shard_map.50 = (bf16[2048,896]{1,0:T(8,128)(2,1)}, f32[16,128]{1,0:T(8,128)}, s32[1]{0:T(128)}, s32[1]{0:T(128)}) custom-call(s32[128,16]{1,0:T(8,128)S(1)} %get-tuple-element.113.tab_s, s32[1,128]{1,0:T(1,128)S(1)} %get-tuple-element.114.cnt_s, f32[14392,128]{1,0:T(8,128)S(1)} %get-tuple-element.115.rows_f, f32[16,128]{1,0:T(8,128)S(1)} %get-tuple-element.116.keys_v), custom_call_target="tpu_custom_call" | custom-call | tf_op jit(solution)/shard_map/pallas_call | solution.py:452
  67.9 0.0 copy-done
  67.9 0.0 copy-done.1
  67.9 0.8 %while.33 = (s32[]{:T(128)}, f32[2048]{0:T(1024)}, bf16[2048,896]{1,0:T(8,128)(2,1)}, f32[1024]{0:T(1024)S(1)}, bf16[1024,896]{1,0:T(8,128)(2,1)S(1)}) while((s32[]{:T(128)}, f32[2048]{0:T(1024)}, bf16[2048,896]{1,0:T(8,128)(2,1)}, f32[1024]{0:T(1024)S(1)}, bf16[1024,896]{1,0:T(8,128)(2,1)S(1)}) %tuple.53), condition=%region_6.7_spmd, body=%region_0.6_spmd | while | flops 2141794 | bytes 33904364 | solution.py:505
Async XLA Ops:
  63.0 4.9 %copy-start = (bf16[1024,896]{1,0:T(8,128)(2,1)S(1)}, bf16[1024,896]{1,0:T(8,128)(2,1)}, u32[]{:S(2)}) copy-start(bf16[1024,896]{1,0:T(8,128)(2,1)} %pay_hbm.1) | copy-start | bytes 5505028
  63.0 4.9 %copy-start.1 = (f32[1024]{0:T(1024)S(1)}, f32[1024]{0:T(1024)}, u32[]{:S(2)}) copy-start(f32[1024]{0:T(1024)} %param.6) | copy-start | bytes 12292

commit v5 on v4

--- a/solution.py
+++ b/solution.py
@@ -358,7 +358,7 @@
     return pl.pallas_call(
         exchange_kernel,
         out_shape=(
-            jax.ShapeDtypeStruct(((OUT + 8) * T, 128), jnp.float32),
+            jax.ShapeDtypeStruct(((OUT + 8) * T + 8, 128), jnp.float32),
             jax.ShapeDtypeStruct((G, 16), jnp.int32),
             jax.ShapeDtypeStruct((OUT // 128, 128), jnp.float32),
             jax.ShapeDtypeStruct((1, 128), jnp.int32),
@@ -368,8 +368,8 @@
         scratch_shapes=[
             pltpu.VMEM((8, 128), jnp.float32),
             pltpu.VMEM((N, W), jnp.bfloat16),
-            pltpu.VMEM((N * T, 128), jnp.float32),
-            pltpu.VMEM((24 * T, 128), jnp.float32),
+            pltpu.VMEM((N * T + 8, 128), jnp.float32),
+            pltpu.VMEM((24 * T + 8, 128), jnp.float32),
             pltpu.VMEM((3 * CHIPS, PART, W), jnp.bfloat16),
             pltpu.VMEM((G, PART, W), jnp.bfloat16),
             pltpu.VMEM((G, PART, W), jnp.bfloat16),
@@ -460,7 +460,7 @@
         in_specs=[smem, smem, vmem, vmem],
         out_specs=(hbm, hbm, hbm, hbm),
         scratch_shapes=[
-            pltpu.VMEM((16 * T, 128), jnp.float32),
+            pltpu.VMEM((16 * T + 8, 128), jnp.float32),
             pltpu.VMEM((OUT, W), jnp.bfloat16),
             pltpu.VMEM((128, W), jnp.bfloat16),
             pltpu.SMEM((1,), jnp.int32),

time: 69 us -> 69 us (level)
  no operation moved by 1% of the time
where the time goes in v5:
time: 69 us; the launch traced here: 68.3 us
  Pallas kernels  66.6 us (97%)
  between operations  0.86 us (1%)
  loops' own time  0.78 us (1%)
    pallas_call x1, Pallas kernels, exchange(): pl.pallas_call(exchange_kernel, out_shape=(jax.ShapeDtypeStruct(((OUT + 8...  61.7 us
    pallas_call x1, Pallas kernels, reorder(): pl.pallas_call(order_kernel, out_shape=(jax.ShapeDtypeStruct((OUT, W), jn...  4.89 us

profile of v5, /device:TPU:1, one launch (start us, length us, event | category | flops | bytes accessed | tf_op | source)
XLA Modules:
  0.0 68.3 jit_solution(14368736484431397874)
XLA Ops:
  0.6 61.7 %shard_map.49 = (f32[14400,128]{1,0:T(8,128)S(1)}, s32[128,16]{1,0:T(8,128)S(1)}, f32[16,128]{1,0:T(8,128)S(1)}, s32[1,128]{1,0:T(1,128)S(1)}) custom-call(f32[8,128]{1,0:T(8,128)} %bitcast.14, bf16[1024,896]{1,0:T(8,128)(2,1)} %pay_hbm.1), custom_call_target="tpu_custom_call" | custom-call | tf_op jit(solution)/shard_map/pallas_call | solution.py:358
  62.3 0.0 copy-start
  62.4 0.0 copy-start.1
  62.4 4.9 %shard_map.50 = (bf16[2048,896]{1,0:T(8,128)(2,1)}, f32[16,128]{1,0:T(8,128)}, s32[1]{0:T(128)}, s32[1]{0:T(128)}) custom-call(s32[128,16]{1,0:T(8,128)S(1)} %get-tuple-element.113.tab_s, s32[1,128]{1,0:T(1,128)S(1)} %get-tuple-element.114.cnt_s, f32[14400,128]{1,0:T(8,128)S(1)} %get-tuple-element.115.rows_f, f32[16,128]{1,0:T(8,128)S(1)} %get-tuple-element.116.keys_v), custom_call_target="tpu_custom_call" | custom-call | tf_op jit(solution)/shard_map/pallas_call | solution.py:452
  67.3 0.0 copy-done
  67.3 0.0 copy-done.1
  67.3 0.8 %while.33 = (s32[]{:T(128)}, f32[2048]{0:T(1024)}, bf16[2048,896]{1,0:T(8,128)(2,1)}, f32[1024]{0:T(1024)S(1)}, bf16[1024,896]{1,0:T(8,128)(2,1)S(1)}) while((s32[]{:T(128)}, f32[2048]{0:T(1024)}, bf16[2048,896]{1,0:T(8,128)(2,1)}, f32[1024]{0:T(1024)S(1)}, bf16[1024,896]{1,0:T(8,128)(2,1)S(1)}) %tuple.53), condition=%region_6.7_spmd, body=%region_0.6_spmd | while | flops 2141794 | bytes 33904364 | solution.py:505
Async XLA Ops:
  62.3 4.9 %copy-start = (bf16[1024,896]{1,0:T(8,128)(2,1)S(1)}, bf16[1024,896]{1,0:T(8,128)(2,1)}, u32[]{:S(2)}) copy-start(bf16[1024,896]{1,0:T(8,128)(2,1)} %pay_hbm.1) | copy-start | bytes 5505028
  62.4 4.9 %copy-start.1 = (f32[1024]{0:T(1024)S(1)}, f32[1024]{0:T(1024)}, u32[]{:S(2)}) copy-start(f32[1024]{0:T(1024)} %param.6) | copy-start | bytes 12292
